TPU v7x, 32 devices: a whole 2x2x4 slice. The times are simulated.
32 devices in a mesh: shot: 2 (over x), mp: 16 (over z, y, core).
Axes of the slice: x: 2, y: 2, z: 4, core: 2. Of those that a mesh axis runs over, the one named last changes fastest.
Arguments:
- gradient_parts: float32 [8, 1024, 1024], P('shot', 'mp')
- history_s: bfloat16 [10, 1024, 1024], P(None, 'mp'), may hold values from -6 to 6
- history_y: bfloat16 [10, 1024, 1024], P(None, 'mp'), as said below
Outputs:
- direction: float32 [1024, 1024], P('mp', 'shot')
Inputs may be any that keep to these rules, and one draw needn't show every extreme that they name: In every cell, history_y[i] equals history_s[i] times a factor between 0.5 and 4.
All inputs are finite; a program needn't handle non-finite values.
Results may differ from a plain program's by a relative error of at most 0.0003.
Values sent between devices are 32-bit elements; how exact they have to be, the bound alone decides.
A program may use at most 64 MiB of HBM per device.

v0:
```python
import jax
import jax.numpy as jnp
from jax import lax
from jax.sharding import PartitionSpec as P

M = 10


def from_gram(gradient, steps, changes):
    shape = gradient.shape
    flat_grad = gradient.reshape(-1)
    stacked = jnp.concatenate([steps.reshape(M, -1), changes.reshape(M, -1)], axis=0)
    hist_gram = lax.dot_general(
        stacked, stacked, (((1,), (1,)), ((), ())), preferred_element_type=jnp.float32
    )
    stacked_wide = stacked.astype(jnp.float32)
    cross = jnp.dot(stacked_wide, flat_grad, precision=lax.Precision.HIGHEST)
    grad_sq = jnp.sum(flat_grad * flat_grad)
    top = jnp.concatenate([hist_gram, cross[:, None]], axis=1)
    bottom = jnp.concatenate([cross, grad_sq[None]])[None, :]
    gram = lax.psum(jnp.concatenate([top, bottom], axis=0), ("shot", "mp"))
    coeffs = jnp.zeros((2 * M + 1,), jnp.float32).at[2 * M].set(1.0)
    alphas = [None] * M
    for i in reversed(range(M)):
        rho_i = 1.0 / gram[i, M + i]
        alphas[i] = rho_i * jnp.dot(gram[i], coeffs, precision=lax.Precision.HIGHEST)
        coeffs = coeffs.at[M + i].add(-alphas[i])
    coeffs = coeffs * (gram[M - 1, 2 * M - 1] / gram[2 * M - 1, 2 * M - 1])
    for i in range(M):
        rho_i = 1.0 / gram[i, M + i]
        beta = rho_i * jnp.dot(gram[M + i], coeffs, precision=lax.Precision.HIGHEST)
        coeffs = coeffs.at[i].add(alphas[i] - beta)
    combined = (
        jnp.dot(coeffs[: 2 * M], stacked_wide, precision=lax.Precision.HIGHEST)
        + coeffs[2 * M] * flat_grad
    )
    return -combined.reshape(shape)


def shards(gradient_parts, history_s, history_y):
    partial_grad = jnp.sum(gradient_parts, axis=0)
    columns = partial_grad.shape[1] // lax.axis_size("shot")
    start = lax.axis_index("shot") * columns
    gradient = lax.psum_scatter(partial_grad, "shot", scatter_dimension=1, tiled=True)
    steps = lax.dynamic_slice_in_dim(history_s, start, columns, 2)
    changes = lax.dynamic_slice_in_dim(history_y, start, columns, 2)
    result = from_gram(gradient, steps, changes)
    return result


def solution(mesh):
    placed = (P("shot", "mp", None), P(None, "mp", None), P(None, "mp", None))
    return jax.shard_map(
        shards, mesh=mesh, in_specs=placed, out_specs=P("mp", "shot"), check_vma=False
    )
```

profile of v0, /device:TPU:0, one launch (start us, length us, event | category | flops | bytes accessed | tf_op | source)
XLA Modules:
  0.0 115.3 jit_solution(11096996644224984904)
XLA Ops:
  6.5 2.1 %reduce_sum.18 = f32[64,1024]{1,0:T(8,128)} reduce(f32[4,64,1024]{2,1,0:T(8,128)} %param.45, f32[]{:T(128)} %constant.493.clone.1), dimensions={0}, to_apply=%region_0.0 | reduce | flops 196608 | bytes 1310724 | tf_op jit(solution)/shard_map/reduce_sum | solution.py:41
  8.7 1.2 %constant_dynamic-slice_fusion = (bf16[10,64,512]{2,1,0:T(8,128)(2,1)S(1)}, bf16[10,64,512]{2,1,0:T(8,128)(2,1)S(1)}) fusion(bf16[10,64,1024]{2,1,0:T(8,128)(2,1)S(1)} %copy-done.1, s32[]{:T(128)S(6)} %select_n.4, bf16[10,64,1024]{2,1,0:T(8,128)(2,1)} %param.46), kind=kLoop, calls=%fused_computation.25 | loop fusion | bytes 2621444 | tf_op jit(solution)/shard_map/dynamic_slice | solution.py:46
  10.0 0.6 copy.47
  10.7 0.6 copy.48
  11.3 0.9 fusion.4
  12.2 11.9 %reduce-scatter.2.cloned.1.call-done = f32[64,512]{1,0:T(8,128)} async-done(((f32[64,1024]{1,0:T(8,128)}), f32[64,512]{1,0:T(8,128)}) %reduce-scatter.2.cloned.1.call-update) | async-done | bytes 131088 | tf_op jit(solution)/shard_map/reduce_scatter | solution.py:44
  24.1 1.1 copy.49
  25.2 1.7 %fusion.3 = f32[1,20]{1,0:T(1,128)S(1)} fusion(f32[32768,1]{0,1:T(1,128)S(1)} %bitcast.66, bf16[10,32768]{1,0:T(8,128)(2,1)S(1)} %bitcast.62, bf16[10,32768]{1,0:T(8,128)(2,1)S(1)} %bitcast.59), kind=kOutput, calls=%fused_computation.71 | convolution fusion | flops 10485760 | bytes 1441872 | tf_op jit(solution)/shard_map/dot_general | solution.py:17
  26.9 0.7 multiply_reduce_fusion
  27.6 0.7 maximum_bitcast_fusion
  28.5 39.4 %psum.7 = f32[21,21]{0,1:T(8,128)S(1)} all-reduce(f32[21,21]{0,1:T(8,128)S(1)} %pad_maximum_fusion.1), channel_id=1, replica_groups=mesh['shot'=2,'mp'=16] {'shot','mp'}, use_global_device_ids=true, to_apply=%region_3.0 | all-reduce | flops 441 | bytes 3528 | tf_op jit(solution)/shard_map/psum | solution.py:21
  67.9 0.7 fusion.5
  68.6 0.2 slice_reduce_fusion.19
  68.8 0.5 slice_reduce_fusion
  70.0 0.6 multiply_reduce_fusion.20
  71.8 0.7 multiply_reduce_fusion.19
  73.1 0.2 constant_dynamic-update-slice_fusion.18
  73.9 0.6 multiply_reduce_fusion.18
  75.8 0.6 multiply_reduce_fusion.17
  77.0 0.2 constant_dynamic-update-slice_fusion.16
  77.8 0.7 multiply_reduce_fusion.16
  79.1 0.2 constant_dynamic-update-slice_fusion.15
  79.9 0.6 multiply_reduce_fusion.15
  82.1 0.7 multiply_reduce_fusion.14
  83.4 0.2 constant_dynamic-update-slice_fusion.13
  84.3 0.7 multiply_reduce_fusion.13
  85.7 0.2 constant_dynamic-update-slice_fusion.12
  86.5 0.6 multiply_reduce_fusion.12
  88.5 0.6 multiply_reduce_fusion.11
  91.3 0.6 multiply_reduce_fusion.10
  92.6 0.6 multiply_reduce_fusion.9
  93.8 0.2 constant_dynamic-update-slice_fusion.9
  94.0 0.6 multiply_reduce_fusion.8
  95.2 0.2 constant_dynamic-update-slice_fusion.8
  95.4 0.6 multiply_reduce_fusion.7
  96.6 0.2 constant_dynamic-update-slice_fusion.7
  96.8 0.6 multiply_reduce_fusion.6
  98.0 0.2 constant_dynamic-update-slice_fusion.6
  98.2 0.6 multiply_reduce_fusion.5
  99.5 0.2 constant_dynamic-update-slice_fusion.5
  99.6 0.6 multiply_reduce_fusion.4
  101.0 0.6 multiply_reduce_fusion.3
  102.4 0.6 multiply_reduce_fusion.2
  103.8 0.6 multiply_reduce_fusion.1
  105.2 1.2 %fusion = f32[1,32768]{1,0:T(1,128)S(1)} fusion(f32[21]{0:T(128)S(1)} %constant_dynamic-update-slice_fusion.1, bf16[10,32768]{1,0:T(8,128)(2,1)S(1)} %bitcast.63, bf16[10,32768]{1,0:T(8,128)(2,1)S(1)} %bitcast.60), kind=kOutput, calls=%fused_computation.28 | convolution fusion | flops 10485760 | bytes 1441876 | tf_op jit(solution)/shard_map/dot_general | solution.py:34
  106.4 0.6 slice.407
  107.1 0.7 add_negate_fusion
  107.7 0.7 neg.47
  (24 shorter events, 1.7 us)
Async XLA Ops:
  6.5 2.1 %copy-start.1 = (bf16[10,64,1024]{2,1,0:T(8,128)(2,1)S(1)}, bf16[10,64,1024]{2,1,0:T(8,128)(2,1)}, u32[]{:S(2)}) copy-start(bf16[10,64,1024]{2,1,0:T(8,128)(2,1)} %param.47) | copy-start | bytes 3932164
  6.5 17.5 %reduce-scatter.2.cloned.1.call-start = ((), (), s32[]{:S(2)}) async-start(), calls=%async_computation.1 | async-start | bytes 393216 | tf_op jit(solution)/shard_map/reduce_scatter | solution.py:44
  10.7 0.7 copy-start.2
  24.1 2.9 %copy-start = (f32[64,512]{1,0:T(8,128)S(1)}, f32[64,512]{1,0:T(8,128)}, u32[]{:S(2)}) copy-start(f32[64,512]{1,0:T(8,128)} %reduce-scatter.2.cloned.1.call-done) | copy-start | bytes 393220
Sparse Core Ops, SparseCore 0:
  9.6 14.4 reduce-scatter.1
where the time goes:
time: 116 us; the launch traced here: 115 us
  blocking collectives  39.4 us (34%)
  between operations  34.3 us (30%)
  other arithmetic  19.3 us (17%)
  waiting for transfers between devices  11.9 us (10%)
  local copies, waits for them, and re-layouts  6.54 us (6%)
  matrix products  3.83 us (3%)
    psum x1, blocking collectives, from_gram(): gram = lax.psum(jnp.concatenate([top, bottom], axis=0), ('shot', 'mp'))  39.4 us
    reduce_scatter x1, waiting for transfers between devices, shards(): lax.psum_scatter(partial_grad, 'shot', scatter_dimension=1, tiled=True)  11.9 us
    dot_general x10, other arithmetic, from_gram(): jnp.dot(gram[i], coeffs, precision=lax.Precision.HIGHEST)  6.32 us
    dot_general x10, other arithmetic, from_gram(): beta = rho_i * jnp.dot(gram[M + i], coeffs, precision=lax.Precision.HIGHEST)  6.05 us
    unnamed x13, local copies, waits for them, and re-layouts  2.55 us
  transfers between devices with their start and end apart: 1, of which 1 were waited for; matrix products, arithmetic and copies ran while one was open for 3% of the time, Pallas kernels for 0%

commit v1 on v0

--- a/solution.py
+++ b/solution.py
@@ -1,9 +1,20 @@
+import functools
 import jax
 import jax.numpy as jnp
 from jax import lax
 from jax.sharding import PartitionSpec as P
+from jax.lax import psum
 
 M = 10
+
+
+def mark_the_paths(here_x, dev_axis, axis_id):
+    inter = psum(here_x, dev_axis)
+    res = psum(inter, axis_id)
+    return res
+
+
+edit_sheets = functools.partial(mark_the_paths, dev_axis="mp", axis_id="shot")
 
 
 def from_gram(gradient, steps, changes):
@@ -18,7 +29,7 @@
     grad_sq = jnp.sum(flat_grad * flat_grad)
     top = jnp.concatenate([hist_gram, cross[:, None]], axis=1)
     bottom = jnp.concatenate([cross, grad_sq[None]])[None, :]
-    gram = lax.psum(jnp.concatenate([top, bottom], axis=0), ("shot", "mp"))
+    gram = edit_sheets(jnp.concatenate([top, bottom], axis=0))
     coeffs = jnp.zeros((2 * M + 1,), jnp.float32).at[2 * M].set(1.0)
     alphas = [None] * M
     for i in reversed(range(M)):

time: 116 us -> 145 us (1.25)
  blocking collectives: 39.4 us -> 68.1 us
    psum x1 -> x2, blocking collectives: 39.4 us -> 68.1 us  [the longest x1 61 us: mark_the_paths(): inter = psum(here_x, dev_axis)]
  transfers between devices with their start and end apart: 1 -> 1, of which waited for: 1 -> 1; matrix products, arithmetic and copies ran while one was open for 3% -> 2% of each run, Pallas kernels for 0% -> 0%
where the time goes in v1:
time: 145 us; the launch traced here: 144 us
  blocking collectives  68.1 us (47%)
  between operations  34.3 us (24%)
  other arithmetic  19.3 us (13%)
  waiting for transfers between devices  11.9 us (8%)
  local copies, waits for them, and re-layouts  6.54 us (5%)
  matrix products  3.83 us (3%)
    psum x1, blocking collectives, mark_the_paths(): inter = psum(here_x, dev_axis)  61 us
    reduce_scatter x1, waiting for transfers between devices, shards(): lax.psum_scatter(partial_grad, 'shot', scatter_dimension=1, tiled=True)  11.9 us
    psum x1, blocking collectives, mark_the_paths(): res = psum(inter, axis_id)  7.11 us
    dot_general x10, other arithmetic, from_gram(): jnp.dot(gram[i], coeffs, precision=lax.Precision.HIGHEST)  6.32 us
    dot_general x10, other arithmetic, from_gram(): beta = rho_i * jnp.dot(gram[M + i], coeffs, precision=lax.Precision.HIGHEST)  6.05 us
  transfers between devices with their start and end apart: 1, of which 1 were waited for; matrix products, arithmetic and copies ran while one was open for 2% of the time, Pallas kernels for 0%

profile of v1, /device:TPU:0, one launch (start us, length us, event | category | flops | bytes accessed | tf_op | source)
XLA Modules:
  0.0 144.0 jit_solution(866326971893934489)
XLA Ops:
  6.5 2.1 %reduce_sum.18 = f32[64,1024]{1,0:T(8,128)} reduce(f32[4,64,1024]{2,1,0:T(8,128)} %param.45, f32[]{:T(128)} %constant.493.clone.1), dimensions={0}, to_apply=%region_0.0 | reduce | flops 196608 | bytes 1310724 | tf_op jit(solution)/shard_map/reduce_sum | solution.py:52
  8.7 1.2 constant_dynamic-slice_fusion
  10.0 0.6 copy.47
  10.7 0.6 copy.48
  11.3 0.9 fusion.4
  12.2 11.9 %reduce-scatter.2.cloned.1.call-done = f32[64,512]{1,0:T(8,128)} async-done(((f32[64,1024]{1,0:T(8,128)}), f32[64,512]{1,0:T(8,128)}) %reduce-scatter.2.cloned.1.call-update) | async-done | bytes 131088 | tf_op jit(solution)/shard_map/reduce_scatter | solution.py:55
  24.1 1.1 copy.49
  25.2 1.7 %fusion.3 = f32[1,20]{1,0:T(1,128)S(1)} fusion(f32[32768,1]{0,1:T(1,128)S(1)} %bitcast.66, bf16[10,32768]{1,0:T(8,128)(2,1)S(1)} %bitcast.62, bf16[10,32768]{1,0:T(8,128)(2,1)S(1)} %bitcast.59), kind=kOutput, calls=%fused_computation.71 | convolution fusion | flops 10485760 | bytes 1441872 | tf_op jit(solution)/shard_map/dot_general | solution.py:28
  26.9 0.7 multiply_reduce_fusion
  27.6 0.7 maximum_bitcast_fusion
  28.5 61.0 %psum.14 = f32[21,21]{0,1:T(8,128)S(1)} all-reduce(f32[21,21]{0,1:T(8,128)S(1)} %pad_maximum_fusion.1), channel_id=1, replica_groups=mesh['shot'=2,'mp'=16] {'mp'}, use_global_device_ids=true, to_apply=%region_3.0 | all-reduce | flops 441 | bytes 3528 | tf_op jit(solution)/shard_map/psum | solution.py:12
  89.5 7.1 %psum.15 = f32[21,21]{0,1:T(8,128)S(1)} all-reduce(f32[21,21]{0,1:T(8,128)S(1)} %psum.14), channel_id=1, replica_groups=mesh['shot'=2,'mp'=16] {'shot'}, use_global_device_ids=true, to_apply=%region_4.0 | all-reduce | flops 441 | bytes 3528 | tf_op jit(solution)/shard_map/psum | solution.py:13
  96.6 0.7 fusion.5
  97.3 0.2 slice_reduce_fusion.19
  97.5 0.5 slice_reduce_fusion
  98.7 0.6 multiply_reduce_fusion.20
  100.6 0.7 multiply_reduce_fusion.19
  101.9 0.2 constant_dynamic-update-slice_fusion.18
  102.6 0.6 multiply_reduce_fusion.18
  103.8 0.2 constant_dynamic-update-slice_fusion.17
  104.6 0.6 multiply_reduce_fusion.17
  105.7 0.2 constant_dynamic-update-slice_fusion.16
  106.5 0.7 multiply_reduce_fusion.16
  107.8 0.2 constant_dynamic-update-slice_fusion.15
  108.7 0.6 multiply_reduce_fusion.15
  109.9 0.2 constant_dynamic-update-slice_fusion.14
  110.8 0.7 multiply_reduce_fusion.14
  112.2 0.2 constant_dynamic-update-slice_fusion.13
  113.0 0.7 multiply_reduce_fusion.13
  114.4 0.2 constant_dynamic-update-slice_fusion.12
  115.2 0.6 multiply_reduce_fusion.12
  116.5 0.2 constant_dynamic-update-slice_fusion.11
  117.3 0.6 multiply_reduce_fusion.11
  118.5 0.2 constant_dynamic-update-slice_fusion.10
  120.0 0.6 multiply_reduce_fusion.10
  121.3 0.6 multiply_reduce_fusion.9
  122.7 0.6 multiply_reduce_fusion.8
  124.1 0.6 multiply_reduce_fusion.7
  125.5 0.6 multiply_reduce_fusion.6
  126.9 0.6 multiply_reduce_fusion.5
  128.3 0.6 multiply_reduce_fusion.4
  129.8 0.6 multiply_reduce_fusion.3
  131.2 0.6 multiply_reduce_fusion.2
  132.6 0.6 multiply_reduce_fusion.1
  134.0 1.2 fusion
  135.2 0.6 slice.407
  135.8 0.7 add_negate_fusion
  136.5 0.7 neg.47
  (25 shorter events, 1.9 us)
Async XLA Ops:
  6.5 2.1 %copy-start.1 = (bf16[10,64,1024]{2,1,0:T(8,128)(2,1)S(1)}, bf16[10,64,1024]{2,1,0:T(8,128)(2,1)}, u32[]{:S(2)}) copy-start(bf16[10,64,1024]{2,1,0:T(8,128)(2,1)} %param.47) | copy-start | bytes 3932164
  6.5 17.5 %reduce-scatter.2.cloned.1.call-start = ((), (), s32[]{:S(2)}) async-start(), calls=%async_computation.1 | async-start | bytes 393216 | tf_op jit(solution)/shard_map/reduce_scatter | solution.py:55
  10.7 0.7 copy-start.2
  24.1 2.9 %copy-start = (f32[64,512]{1,0:T(8,128)S(1)}, f32[64,512]{1,0:T(8,128)}, u32[]{:S(2)}) copy-start(f32[64,512]{1,0:T(8,128)} %reduce-scatter.2.cloned.1.call-done) | copy-start | bytes 393220
Sparse Core Ops, SparseCore 0:
  9.6 14.4 reduce-scatter.1
